TPU v7x, 32 devices: a whole 2x2x4 slice. The times are simulated.
32 devices in a mesh: ctx: 8 (over z, x), dp: 4 (over y, core).
Axes of the slice: x: 2, y: 2, z: 4, core: 2. Of those that a mesh axis runs over, the one named last changes fastest.
Arguments:
- head_input: bfloat16 [8192, 4096], P(('dp', 'ctx')), parts along dimension 0, may hold values from -6 to 6
- gate_input: bfloat16 [8192, 4096], P(('dp', 'ctx')), parts along dimension 0, may hold values from -6 to 6
- write_vector: bfloat16 [8192, 128], P(('dp', 'ctx')), parts along dimension 0, may hold values from -2.5 to 2.5
- read_vector: bfloat16 [8192, 128], P(('dp', 'ctx')), parts along dimension 0, may hold values from -2.5 to 2.5
- increment_preactivation: bfloat16 [8192, 64], P(('dp', 'ctx')), parts along dimension 0, may hold values from -2 to 8
- step_bias: float32 [64], replicated, may hold values from -1 to 0.5
- decay_log: float32 [64], replicated, may hold values from -9.3 to -2.3
- skip_gain: float32 [64], replicated, may hold values from 0.5 to 1.5
- norm_weight: float32 [4096], replicated, may hold values from 0.5 to 1.5
- doc_starts: int32 [64], P(('dp', 'ctx')), parts along dimension 0, may hold values from 0 to 1, as said below
- block_order: int32 [64], P(('dp', 'ctx')), parts along dimension 0, may hold values from 0 to 15, as said below
Outputs:
- packed_out: bfloat16 [8192, 4096], P(('dp', 'ctx')), parts along dimension 0
There are 4 independent parts, one for each index of `dp`. A program takes and returns all parts, laid end to end along the dimension named above; an argument that names none is the same for every part. Nothing has to cross between parts.
Inputs may be any that keep to these rules, and one draw needn't show every extreme that they name: `doc_starts`: block 0 starts a document; no document is longer than 128 blocks. `block_order`: a permutation of the block indices that keeps each document's blocks together and in their order.
All inputs are finite; a program needn't handle non-finite values.
Results may differ from a plain program's by a relative error of at most 0.0085.
Values may be sent and summed in bfloat16 or wider, within the bound.
A program may use at most 128 MiB of HBM per device.

v0:
```python
import functools

import jax
import jax.numpy as jnp
from jax import lax
from jax.experimental import pallas as pl
from jax.experimental.pallas import tpu as pltpu
from jax.sharding import PartitionSpec as P

HEAD_DIM = 64
GROUP = 128
CHUNK = 8
WIDE = CHUNK * HEAD_DIM
EXTRA = 16

highest = lax.Precision.HIGHEST
VM = pl.BlockSpec(memory_space=pltpu.VMEM)
SM = pl.BlockSpec(memory_space=pltpu.SMEM)


def transposed(v):
    rows, cols = v.shape
    if cols < 128:
        v = jnp.concatenate([v, jnp.zeros((rows, 128 - cols), v.dtype)], axis=1)
    return v.T[:cols]


def lower_mask():
    row = lax.broadcasted_iota(jnp.int32, (GROUP, GROUP), 0)
    col = lax.broadcasted_iota(jnp.int32, (GROUP, GROUP), 1)
    return row >= col


def step_terms(logit_ref, bias_ref, dlog_ref):
    v = logit_ref[...].astype(jnp.float32) + bias_ref[...]
    dt = jnp.maximum(v, 0.0) + jnp.log(1.0 + jnp.exp(-jnp.abs(v)))
    return dt, -dt * jnp.exp(dlog_ref[...])


def spread(v):
    rows = v.shape[0]
    first = lax.broadcasted_iota(jnp.int32, (rows, 128), 1) < HEAD_DIM
    return jnp.concatenate(
        [
            jnp.where(first, v[:, k : k + 1], v[:, k + 1 : k + 2])
            for k in range(0, CHUNK, 2)
        ],
        axis=1,
    )


def prepare(logit_ref, bias_ref, dlog_ref, write_ref, cum_s, dt_s, write_t):
    heads = bias_ref.shape[1]
    dt, fall = step_terms(logit_ref, bias_ref, dlog_ref)
    tri = lower_mask().astype(jnp.float32)
    cums = []
    for g in range(write_t.shape[0]):
        rows = slice(g * GROUP, (g + 1) * GROUP)
        cum = jnp.dot(tri, fall[rows], precision=highest, preferred_element_type=jnp.float32)
        cums.append(cum)
        for c in range(heads // CHUNK):
            cum_s[g, c] = cum[:, c * CHUNK : (c + 1) * CHUNK]
            dt_s[g, c] = dt[rows, c * CHUNK : (c + 1) * CHUNK]
        write_t[g] = write_ref[rows, :].astype(jnp.float32).T.astype(jnp.bfloat16)
    return dt, cums


def group_state(g, c, x, cum_s, dt_s, write_t):
    cum = cum_s[g, c]
    last = cum[GROUP - 1 : GROUP]
    tail = jnp.exp(last - cum) * dt_s[g, c]
    scaled = (x.astype(jnp.float32) * spread(tail)).astype(jnp.bfloat16)
    state = jnp.dot(write_t[g], scaled, preferred_element_type=jnp.float32)
    return state, spread(jnp.exp(last))


def state_kernel(
    x_ref, logit_ref, write_ref, bias_ref, dlog_ref, starts_ref, order_ref, out_ref, cum_s, dt_s, write_t
):
    groups = write_t.shape[0]
    prepare(logit_ref, bias_ref, dlog_ref, write_ref, cum_s, dt_s, write_t)
    parts, _, width = out_ref.shape
    chunks = cum_s.shape[1]
    per = width // WIDE

    def one(c, carry):
        cols = pl.ds(pl.multiple_of(c * WIDE, WIDE), WIDE)
        total, decay = None, None
        for g in range(groups):
            x = x_ref[g * GROUP : (g + 1) * GROUP, cols]
            state, last = group_state(g, c, x, cum_s, dt_s, write_t)
            keep = 1.0 - starts_ref[g].astype(jnp.float32)
            factor = keep * last
            total = state if total is None else factor * total + state
            decay = factor if decay is None else factor * decay
        coarse = decay.astype(jnp.bfloat16)
        fine = (decay - coarse.astype(jnp.float32)).astype(jnp.bfloat16)
        row = lax.broadcasted_iota(jnp.int32, (EXTRA, WIDE), 0)
        lane = lax.broadcasted_iota(jnp.int32, (EXTRA, WIDE), 1)
        order = jnp.zeros((EXTRA, WIDE), jnp.float32)
        for g in range(groups):
            order = jnp.where(lane == g, order_ref[g].astype(jnp.float32), order)
        extra = jnp.where(
            row == 0,
            coarse.astype(jnp.float32),
            jnp.where(row == 1, fine.astype(jnp.float32), order),
        )
        full = jnp.concatenate([total, extra], axis=0).astype(jnp.bfloat16)
        if parts == 1:
            out_ref[0, :, cols] = full
        else:
            into = pl.ds(pl.multiple_of((c % per) * WIDE, WIDE), WIDE)
            out_ref[c // per, :, into] = full
        return carry

    lax.fori_loop(0, chunks, one, 0)


def scan_kernel(in_ref, out_ref):
    parts, _, width = in_ref.shape
    state = jnp.zeros((GROUP, width), jnp.float32)
    for s in range(parts):
        out_ref[s] = state.astype(jnp.bfloat16)
        extra = in_ref[s, GROUP : GROUP + EXTRA, :].astype(jnp.float32)
        decay = extra[0:1] + extra[1:2]
        state = decay * state + in_ref[s, :GROUP, :].astype(jnp.float32)


def gated_kernel(
    x_ref,
    gate_ref,
    logit_ref,
    write_ref,
    read_ref,
    entry_ref,
    bias_ref,
    dlog_ref,
    gain_ref,
    starts_ref,
    out_ref,
    cum_s,
    dt_s,
    write_t,
    cum_t,
    dt_t,
    gain_s,
    score_s,
):
    groups, chunks = cum_s.shape[:2]
    dt, cums = prepare(logit_ref, bias_ref, dlog_ref, write_ref, cum_s, dt_s, write_t)
    mask = lower_mask()
    for g in range(groups):
        rows = slice(g * GROUP, (g + 1) * GROUP)
        ct = transposed(cums[g])
        dtt = transposed(dt[rows])
        for c in range(chunks):
            cum_t[g, c] = ct[c * CHUNK : (c + 1) * CHUNK]
            dt_t[g, c] = dtt[c * CHUNK : (c + 1) * CHUNK]
        score = jnp.dot(read_ref[rows, :], write_t[g], preferred_element_type=jnp.float32)
        score_s[g] = jnp.where(mask, score, 0.0)
    for c in range(chunks):
        gain_s[c] = jnp.broadcast_to(gain_ref[:, c * CHUNK : (c + 1) * CHUNK], (8, CHUNK))
    parts, _, width = out_ref.shape
    per = width // WIDE
    first = lax.broadcasted_iota(jnp.int32, (GROUP, 128), 1) < HEAD_DIM

    def one(c, carry):
        cols = pl.ds(pl.multiple_of(c * WIDE, WIDE), WIDE)
        into = pl.ds(pl.multiple_of((c % per) * WIDE, WIDE), WIDE)
        if entry_ref.shape[0] == 1:
            state = entry_ref[0, :, cols].astype(jnp.float32)
        else:
            state = entry_ref[c // per, :, into].astype(jnp.float32)
        gain = spread(gain_s[c][0:1])
        for g in range(groups):
            rows = slice(g * GROUP, (g + 1) * GROUP)
            x = x_ref[rows, cols]
            keep = 1.0 - starts_ref[g].astype(jnp.float32)
            entering = (keep * state).astype(jnp.bfloat16)
            cum = cum_s[g, c]
            carried = jnp.dot(read_ref[rows, :], entering, preferred_element_type=jnp.float32)
            mixed = carried * spread(jnp.exp(cum)) + gain * x.astype(jnp.float32)
            score = score_s[g]
            ct, dtt = cum_t[g, c], dt_t[g, c]
            pieces = []
            for k in range(0, CHUNK, 2):
                pair = x[:, k * HEAD_DIM : (k + 2) * HEAD_DIM]
                both = []
                for h in (k, k + 1):
                    gap = cum[:, h : h + 1] - ct[h : h + 1]
                    weight = score * jnp.exp(jnp.minimum(gap, 0.0)) * dtt[h : h + 1]
                    both.append(
                        jnp.dot(weight.astype(jnp.bfloat16), pair, preferred_element_type=jnp.float32)
                    )
                pieces.append(jnp.where(first, both[0], both[1]))
            mixed = mixed + jnp.concatenate(pieces, axis=1)
            gate = gate_ref[rows, cols].astype(jnp.float32)
            gated = (mixed * (gate / (1.0 + jnp.exp(-gate)))).astype(jnp.bfloat16)
            if parts == 1:
                out_ref[0, rows, cols] = gated
            else:
                out_ref[c // per, rows, into] = gated
            if g + 1 < groups:
                own, last = group_state(g, c, x, cum_s, dt_s, write_t)
                state = keep * last * state + own
        return carry

    lax.fori_loop(0, chunks, one, 0)


def norm_kernel(in_ref, weight_ref, out_ref):
    parts, rows, width = in_ref.shape
    tile = 32

    def one(r, carry):
        at = pl.ds(pl.multiple_of(r * tile, tile), tile)
        total = jnp.zeros((tile, 1), jnp.float32)
        for s in range(parts):
            v = in_ref[s, at, :].astype(jnp.float32)
            total = total + jnp.sum(v * v, axis=1, keepdims=True)
        scale = lax.rsqrt(total * (1.0 / (parts * width)) + 1e-05)
        for s in range(parts):
            v = in_ref[s, at, :].astype(jnp.float32)
            w = weight_ref[:, s * width : (s + 1) * width]
            out_ref[at, s * width : (s + 1) * width] = (v * scale * w).astype(jnp.bfloat16)
        return carry

    lax.fori_loop(0, rows // tile, one, 0)


def local(
    head_input,
    gate_input,
    write_vector,
    read_vector,
    increment_preactivation,
    step_bias,
    decay_log,
    skip_gain,
    norm_weight,
    doc_starts,
    block_order,
):
    devices = lax.axis_size("ctx")
    rows, features = head_input.shape
    heads = step_bias.shape[0]
    groups = rows // GROUP
    chunks = heads // CHUNK
    width = features // devices
    state_size = write_vector.shape[1]
    direct = width % WIDE == 0
    parts = devices if direct else 1
    limit = pltpu.CompilerParams(vmem_limit_bytes=48 * 1024 * 1024)
    common = [
        pltpu.VMEM((groups, chunks, GROUP, CHUNK), jnp.float32),
        pltpu.VMEM((groups, chunks, GROUP, CHUNK), jnp.float32),
        pltpu.VMEM((groups, state_size, GROUP), jnp.bfloat16),
    ]
    bias, dlog, gain = (v.reshape(1, -1) for v in (step_bias, decay_log, skip_gain))

    def to_owners(v):
        if not direct:
            v = v.reshape(v.shape[1], devices, width).transpose(1, 0, 2)
        return lax.all_to_all(v, "ctx", split_axis=0, concat_axis=0, tiled=True)

    def joined(v):
        if not direct:
            v = v.transpose(1, 0, 2).reshape(1, v.shape[1], features)
        return v

    ends = pl.pallas_call(
        state_kernel,
        out_shape=jax.ShapeDtypeStruct((parts, state_size + EXTRA, features // parts), jnp.bfloat16),
        in_specs=[VM] * 5 + [SM] * 2,
        out_specs=VM,
        scratch_shapes=common,
        compiler_params=limit,
        name="end_states",
    )(head_input, increment_preactivation, write_vector, bias, dlog, doc_starts, block_order)
    ends = to_owners(ends)
    all_order = ends[:, state_size + 2, :groups].astype(jnp.int32).reshape(-1)
    entry = pl.pallas_call(
        scan_kernel,
        out_shape=jax.ShapeDtypeStruct((devices, state_size, width), jnp.bfloat16),
        in_specs=[VM],
        out_specs=VM,
        compiler_params=limit,
        name="scan_states",
    )(ends)
    entry = joined(lax.all_to_all(entry, "ctx", split_axis=0, concat_axis=0, tiled=True))
    gated = pl.pallas_call(
        gated_kernel,
        out_shape=jax.ShapeDtypeStruct((parts, rows, features // parts), jnp.bfloat16),
        in_specs=[VM] * 9 + [SM],
        out_specs=VM,
        scratch_shapes=common
        + [
            pltpu.VMEM((groups, chunks, CHUNK, GROUP), jnp.float32),
            pltpu.VMEM((groups, chunks, CHUNK, GROUP), jnp.float32),
            pltpu.VMEM((chunks, 8, CHUNK), jnp.float32),
            pltpu.VMEM((groups, GROUP, GROUP), jnp.float32),
        ],
        compiler_params=limit,
        name="gated",
    )(
        head_input,
        gate_input,
        increment_preactivation,
        write_vector,
        read_vector,
        entry,
        bias,
        dlog,
        gain,
        doc_starts,
    )
    gated = to_owners(gated)
    blocks = gated.reshape(devices * groups, GROUP, width)[all_order]
    packed = lax.all_to_all(
        blocks.reshape(devices, rows, width), "ctx", split_axis=0, concat_axis=0, tiled=True
    )
    return pl.pallas_call(
        norm_kernel,
        out_shape=jax.ShapeDtypeStruct((rows, features), jnp.bfloat16),
        in_specs=[VM] * 2,
        out_specs=VM,
        compiler_params=limit,
        name="norm",
    )(joined(packed), norm_weight.reshape(1, -1))


def solution(mesh):
    return jax.shard_map(
        local,
        mesh=mesh,
        in_specs=(
            P(("dp", "ctx"), None),
            P(("dp", "ctx"), None),
            P(("dp", "ctx"), None),
            P(("dp", "ctx"), None),
            P(("dp", "ctx"), None),
            P(),
            P(),
            P(),
            P(),
            P(("dp", "ctx")),
            P(("dp", "ctx")),
        ),
        out_specs=P(("dp", "ctx"), None),
        check_vma=False,
    )
```

profile of v0, /device:TPU:0, one launch (start us, length us, event | category | flops | bytes accessed | tf_op | source)
XLA Modules:
  0.0 197.9 jit_solution(12029471757610194146)
XLA Ops:
  0.0 0.9 copy.15.logit_ref
  0.9 0.0 copy-start
  0.9 1.6 copy-done
  2.5 0.0 copy-start.2
  2.5 0.8 copy-done.2
  3.3 0.0 copy-start.5
  3.3 0.7 copy-done.5
  4.0 0.0 copy-start.7
  4.0 0.7 copy-done.7
  4.6 0.0 copy-start.9
  4.6 0.7 copy-done.9
  5.3 0.0 copy-start.11
  5.3 0.7 copy-done.11
  5.9 6.1 %end_states.1 = bf16[8,144,512]{2,1,0:T(8,128)(2,1)S(1)} custom-call(bf16[256,4096]{1,0:T(8,128)(2,1)S(1)} %copy-done, bf16[256,64]{1,0:T(8,128)(2,1)S(1)} %copy.15.logit_ref, bf16[256,128]{1,0:T(8,128)(2,1)S(1)} %copy-done.2, f32[1,64]{1,0:T(1,128)S(1)} %bitcast.9, f32[1,64]{1,0:T(1,128)S(1)} %bitcast.11, s32[2]{0:T(128)S(1)} %copy-done.9, s32[2]{0:T(128)S(1)} %copy-done.11), custom_call_target="tpu_custom_call" | custom-call | tf_op jit(solution)/shard_map/end_states/pallas_call | solution.py:271
  12.0 36.0 %all_to_all.20.in_ref = bf16[8,144,512]{2,1,0:T(8,128)(2,1)S(1)} all-to-all(bf16[8,144,512]{2,1,0:T(8,128)(2,1)S(1)} %end_states.1), channel_id=1, replica_groups=mesh['ctx'=8,'dp'=4] {'ctx'}, dimensions={0} | all-to-all | bytes 2359296 | tf_op jit(solution)/shard_map/all_to_all | solution.py:264
  48.0 0.0 copy-start.1
  48.0 0.0 copy-start.3
  48.0 0.0 copy-start.6
  48.0 0.0 copy-start.8
  48.0 0.0 copy-start.10
  48.0 0.0 copy-start.12
  48.0 0.2 scan_states.1
  48.2 28.8 %all_to_all.21.entry_ref = bf16[8,128,512]{2,1,0:T(8,128)(2,1)S(1)} all-to-all(bf16[8,128,512]{2,1,0:T(8,128)(2,1)S(1)} %scan_states.1), channel_id=1, replica_groups=mesh['ctx'=8,'dp'=4] {'ctx'}, dimensions={0} | all-to-all | bytes 2097152 | tf_op jit(solution)/shard_map/all_to_all | solution.py:290
  77.0 0.0 copy-done.1
  77.0 0.0 copy-done.3
  77.0 0.0 copy-done.6
  77.0 0.0 copy-done.8
  77.1 0.0 copy-done.10
  77.1 0.0 copy-done.12
  77.1 12.4 %gated.1 = bf16[8,256,512]{2,1,0:T(8,128)(2,1)} custom-call(bf16[256,4096]{1,0:T(8,128)(2,1)S(1)} %copy-done.1, bf16[256,4096]{1,0:T(8,128)(2,1)} %gate_ref.1, bf16[256,64]{1,0:T(8,128)(2,1)S(1)} %copy.15.logit_ref, bf16[256,128]{1,0:T(8,128)(2,1)S(1)} %copy-done.2, bf16[256,128]{1,0:T(8,128)(2,1)S(1)} %copy-done.3, ...), custom_call_target="tpu_custom_call" | custom-call | tf_op jit(solution)/shard_map/gated/pallas_call | solution.py:291
  89.5 3.6 %all-to-all-start.2 = ((bf16[8,256,512]{2,1,0:T(8,128)(2,1)}), bf16[8,256,512]{2,1,0:T(8,128)(2,1)S(1)}, u32[]{:S(2)}, u32[]{:S(2)}) async-start(bf16[8,256,512]{2,1,0:T(8,128)(2,1)} %gated.1), calls=%async_computation.2 | async-start | bytes 4194304 | tf_op jit(solution)/shard_map/all_to_all | solution.py:264
  93.2 0.1 reshape.47
  93.2 47.7 %all-to-all-done.2 = bf16[8,256,512]{2,1,0:T(8,128)(2,1)S(1)} async-done(((bf16[8,256,512]{2,1,0:T(8,128)(2,1)}), bf16[8,256,512]{2,1,0:T(8,128)(2,1)S(1)}, u32[]{:S(2)}, u32[]{:S(2)}) %all-to-all-start.2) | async-done | bytes 2097184 | tf_op jit(solution)/shard_map/all_to_all | solution.py:264
  141.0 2.0 %gather_fusion = bf16[16,128,512]{2,1,0:T(8,128)(2,1)} fusion(bf16[16,128,512]{2,1,0:T(8,128)(2,1)S(1)} %bitcast.14, s32[1024]{0:T(1024)S(1)} %pad_clamp_fusion), kind=kCustom, calls=%fused_computation | custom fusion | bytes 4194368 | tf_op jit(solution)/shard_map/gather | solution.py:318
  143.0 0.0 copy-start.4
  143.0 52.1 %all_to_all.22.in_ref = bf16[8,256,512]{2,1,0:T(8,128)(2,1)S(1)} all-to-all(bf16[8,256,512]{2,1,0:T(8,128)(2,1)} %bitcast.15), channel_id=1, replica_groups=mesh['ctx'=8,'dp'=4] {'ctx'}, dimensions={0} | all-to-all | bytes 4194304 | tf_op jit(solution)/shard_map/all_to_all | solution.py:319
  195.1 0.0 copy-done.4
  195.1 2.8 %norm.1 = bf16[256,4096]{1,0:T(8,128)(2,1)} custom-call(bf16[8,256,512]{2,1,0:T(8,128)(2,1)S(1)} %all_to_all.22.in_ref, f32[1,4096]{1,0:T(1,128)S(1)} %bitcast.8), custom_call_target="tpu_custom_call" | custom-call | tf_op jit(solution)/shard_map/norm/pallas_call | solution.py:322
  (3 shorter events, 0.0 us)
Async XLA Ops:
  0.9 1.6 copy-start
  2.5 0.8 copy-start.2
  3.3 0.7 copy-start.5
  4.0 0.7 copy-start.7
  4.6 0.7 copy-start.9
  5.3 0.7 copy-start.11
  48.0 29.0 %copy-start.1 = (bf16[256,4096]{1,0:T(8,128)(2,1)S(1)}, bf16[256,4096]{1,0:T(8,128)(2,1)}, u32[]{:S(2)}) copy-start(bf16[256,4096]{1,0:T(8,128)(2,1)} %x_ref.3) | copy-start | bytes 6291460
  48.0 29.0 %copy-start.3 = (bf16[256,128]{1,0:T(8,128)(2,1)S(1)}, bf16[256,128]{1,0:T(8,128)(2,1)}, u32[]{:S(2)}) copy-start(bf16[256,128]{1,0:T(8,128)(2,1)} %read_ref.1) | copy-start | bytes 196612
  48.0 29.0 %copy-start.6 = (f32[64]{0:T(128)S(1)}, f32[64]{0:T(128)}, u32[]{:S(2)}) copy-start(f32[64]{0:T(128)} %param.16) | copy-start | bytes 772
  48.0 29.1 %copy-start.8 = (f32[64]{0:T(128)S(1)}, f32[64]{0:T(128)}, u32[]{:S(2)}) copy-start(f32[64]{0:T(128)} %param.17) | copy-start | bytes 772
  48.0 29.1 %copy-start.10 = (s32[2]{0:T(128)S(1)}, s32[2]{0:T(128)}, u32[]{:S(2)}) copy-start(s32[2]{0:T(128)} %starts_ref.3) | copy-start | bytes 28
  48.0 29.1 %copy-start.12 = (f32[64]{0:T(128)S(1)}, f32[64]{0:T(128)}, u32[]{:S(2)}) copy-start(f32[64]{0:T(128)} %param.18) | copy-start | bytes 772
  89.5 51.5 %all-to-all-start.2 = ((bf16[8,256,512]{2,1,0:T(8,128)(2,1)}), bf16[8,256,512]{2,1,0:T(8,128)(2,1)S(1)}, u32[]{:S(2)}, u32[]{:S(2)}) async-start(bf16[8,256,512]{2,1,0:T(8,128)(2,1)} %gated.1), calls=%async_computation.2 | async-start | bytes 4194304 | tf_op jit(solution)/shard_map/all_to_all | solution.py:264
  143.0 52.1 %copy-start.4 = (f32[4096]{0:T(1024)S(1)}, f32[4096]{0:T(1024)}, u32[]{:S(2)}) copy-start(f32[4096]{0:T(1024)} %param.19) | copy-start | bytes 49156
where the time goes:
time: 198 us
  blocking collectives  117 us (59%)
  waiting for transfers between devices  47.7 us (24%)
  Pallas kernels  21.5 us (11%)
  local copies, waits for them, and re-layouts  8.03 us (4%)
  starting transfers between devices  3.6 us (2%)
    all_to_all x1, blocking collectives, local(): lax.all_to_all(blocks.reshape(devices, rows, width), 'ctx', split_axis=0,...  52.1 us
    all_to_all x1, waiting for transfers between devices, to_owners(): return lax.all_to_all(v, 'ctx', split_axis=0, concat_axis=0, tiled=True)  47.7 us
    all_to_all x1, blocking collectives, to_owners(): return lax.all_to_all(v, 'ctx', split_axis=0, concat_axis=0, tiled=True)  36 us
    all_to_all x1, blocking collectives, local(): lax.all_to_all(entry, 'ctx', split_axis=0, concat_axis=0, tiled=True)  28.8 us
    pallas_call x1, Pallas kernels, local(): pl.pallas_call(gated_kernel, out_shape=jax.ShapeDtypeStruct((parts, rows,...  12.4 us
    pallas_call x1, Pallas kernels, local(): pl.pallas_call(state_kernel, out_shape=jax.ShapeDtypeStruct((parts, state...  6.07 us
    unnamed x27, local copies, waits for them, and re-layouts  5.95 us
  transfers between devices with their start and end apart: 1, of which 1 were waited for; matrix products, arithmetic and copies ran while one was open for 0% of the time, Pallas kernels for 0%

commit v1 on v0

--- a/solution.py
+++ b/solution.py
@@ -126,25 +126,8 @@
         state = decay * state + in_ref[s, :GROUP, :].astype(jnp.float32)
 
 
-def gated_kernel(
-    x_ref,
-    gate_ref,
-    logit_ref,
-    write_ref,
-    read_ref,
-    entry_ref,
-    bias_ref,
-    dlog_ref,
-    gain_ref,
-    starts_ref,
-    out_ref,
-    cum_s,
-    dt_s,
-    write_t,
-    cum_t,
-    dt_t,
-    gain_s,
-    score_s,
+def gated_setup(
+    logit_ref, bias_ref, dlog_ref, write_ref, read_ref, gain_ref, cum_s, dt_s, write_t, cum_t, dt_t, gain_s, score_s
 ):
     groups, chunks = cum_s.shape[:2]
     dt, cums = prepare(logit_ref, bias_ref, dlog_ref, write_ref, cum_s, dt_s, write_t)
@@ -160,52 +143,236 @@
         score_s[g] = jnp.where(mask, score, 0.0)
     for c in range(chunks):
         gain_s[c] = jnp.broadcast_to(gain_ref[:, c * CHUNK : (c + 1) * CHUNK], (8, CHUNK))
+
+
+def gated_chunk(
+    c, state, put, x_ref, gate_ref, read_ref, starts_ref, cum_s, dt_s, write_t, cum_t, dt_t, gain_s, score_s
+):
+    groups = cum_s.shape[0]
+    first = lax.broadcasted_iota(jnp.int32, (GROUP, 128), 1) < HEAD_DIM
+    cols = pl.ds(pl.multiple_of(c * WIDE, WIDE), WIDE)
+    gain = spread(gain_s[c][0:1])
+    for g in range(groups):
+        rows = slice(g * GROUP, (g + 1) * GROUP)
+        x = x_ref[rows, cols]
+        keep = 1.0 - starts_ref[g].astype(jnp.float32)
+        entering = (keep * state).astype(jnp.bfloat16)
+        cum = cum_s[g, c]
+        carried = jnp.dot(read_ref[rows, :], entering, preferred_element_type=jnp.float32)
+        mixed = carried * spread(jnp.exp(cum)) + gain * x.astype(jnp.float32)
+        score = score_s[g]
+        ct, dtt = cum_t[g, c], dt_t[g, c]
+        pieces = []
+        for k in range(0, CHUNK, 2):
+            pair = x[:, k * HEAD_DIM : (k + 2) * HEAD_DIM]
+            both = []
+            for h in (k, k + 1):
+                gap = cum[:, h : h + 1] - ct[h : h + 1]
+                weight = score * jnp.exp(jnp.minimum(gap, 0.0)) * dtt[h : h + 1]
+                both.append(
+                    jnp.dot(weight.astype(jnp.bfloat16), pair, preferred_element_type=jnp.float32)
+                )
+            pieces.append(jnp.where(first, both[0], both[1]))
+        mixed = mixed + jnp.concatenate(pieces, axis=1)
+        gate = gate_ref[rows, cols].astype(jnp.float32)
+        put(g, (mixed * (gate / (1.0 + jnp.exp(-gate)))).astype(jnp.bfloat16))
+        if g + 1 < groups:
+            own, last = group_state(g, c, x, cum_s, dt_s, write_t)
+            state = keep * last * state + own
+
+
+def gated_kernel(
+    x_ref,
+    gate_ref,
+    logit_ref,
+    write_ref,
+    read_ref,
+    entry_ref,
+    bias_ref,
+    dlog_ref,
+    gain_ref,
+    starts_ref,
+    out_ref,
+    *scratch,
+):
+    gated_setup(logit_ref, bias_ref, dlog_ref, write_ref, read_ref, gain_ref, *scratch)
     parts, _, width = out_ref.shape
+    chunks = scratch[0].shape[1]
     per = width // WIDE
-    first = lax.broadcasted_iota(jnp.int32, (GROUP, 128), 1) < HEAD_DIM
 
     def one(c, carry):
         cols = pl.ds(pl.multiple_of(c * WIDE, WIDE), WIDE)
         into = pl.ds(pl.multiple_of((c % per) * WIDE, WIDE), WIDE)
-        if entry_ref.shape[0] == 1:
+        if parts == 1:
             state = entry_ref[0, :, cols].astype(jnp.float32)
         else:
             state = entry_ref[c // per, :, into].astype(jnp.float32)
-        gain = spread(gain_s[c][0:1])
+
+        def put(g, value):
+            rows = slice(g * GROUP, (g + 1) * GROUP)
+            if parts == 1:
+                out_ref[0, rows, cols] = value
+            else:
+                out_ref[c // per, rows, into] = value
+
+        gated_chunk(c, state, put, x_ref, gate_ref, read_ref, starts_ref, *scratch)
+        return carry
+
+    lax.fori_loop(0, chunks, one, 0)
+
+
+def fused_kernel(
+    n,
+    x_ref,
+    gate_ref,
+    logit_ref,
+    write_ref,
+    read_ref,
+    bias_ref,
+    dlog_ref,
+    gain_ref,
+    weight_ref,
+    starts_ref,
+    order_ref,
+    out_ref,
+    fin,
+    fout,
+    total_s,
+    decay_s,
+    made,
+    got,
+    stage,
+    final,
+    chain_send,
+    chain_recv,
+    send1,
+    recv1,
+    send2,
+    recv2,
+    *scratch,
+):
+    cum_s, dt_s, write_t = scratch[:3]
+    groups = cum_s.shape[0]
+    me = lax.axis_index("ctx")
+    offsets = sorted(range(1, n), key=lambda k: abs(k - n // 2))
+    barrier = pltpu.get_barrier_semaphore()
+    for off in range(1, n):
+        pl.semaphore_signal(
+            barrier, inc=1, device_id={"ctx": lax.rem(me + off, n)}, device_id_type=pl.DeviceIdType.MESH
+        )
+    gated_setup(logit_ref, bias_ref, dlog_ref, write_ref, read_ref, gain_ref, *scratch)
+
+    def ends(c, carry):
+        cols = pl.ds(pl.multiple_of(c * WIDE, WIDE), WIDE)
+        total, decay = None, None
         for g in range(groups):
-            rows = slice(g * GROUP, (g + 1) * GROUP)
-            x = x_ref[rows, cols]
-            keep = 1.0 - starts_ref[g].astype(jnp.float32)
-            entering = (keep * state).astype(jnp.bfloat16)
-            cum = cum_s[g, c]
-            carried = jnp.dot(read_ref[rows, :], entering, preferred_element_type=jnp.float32)
-            mixed = carried * spread(jnp.exp(cum)) + gain * x.astype(jnp.float32)
-            score = score_s[g]
-            ct, dtt = cum_t[g, c], dt_t[g, c]
-            pieces = []
-            for k in range(0, CHUNK, 2):
-                pair = x[:, k * HEAD_DIM : (k + 2) * HEAD_DIM]
-                both = []
-                for h in (k, k + 1):
-                    gap = cum[:, h : h + 1] - ct[h : h + 1]
-                    weight = score * jnp.exp(jnp.minimum(gap, 0.0)) * dtt[h : h + 1]
-                    both.append(
-                        jnp.dot(weight.astype(jnp.bfloat16), pair, preferred_element_type=jnp.float32)
-                    )
-                pieces.append(jnp.where(first, both[0], both[1]))
-            mixed = mixed + jnp.concatenate(pieces, axis=1)
-            gate = gate_ref[rows, cols].astype(jnp.float32)
-            gated = (mixed * (gate / (1.0 + jnp.exp(-gate)))).astype(jnp.bfloat16)
-            if parts == 1:
-                out_ref[0, rows, cols] = gated
-            else:
-                out_ref[c // per, rows, into] = gated
-            if g + 1 < groups:
-                own, last = group_state(g, c, x, cum_s, dt_s, write_t)
-                state = keep * last * state + own
+            x = x_ref[g * GROUP : (g + 1) * GROUP, cols]
+            state, last = group_state(g, c, x, cum_s, dt_s, write_t)
+            factor = (1.0 - starts_ref[g].astype(jnp.float32)) * last
+            total = state if total is None else factor * total + state
+            decay = factor if decay is None else factor * decay
+        total_s[c] = total
+        decay_s[c] = jnp.broadcast_to(decay, (8, WIDE))
         return carry
 
-    lax.fori_loop(0, chunks, one, 0)
+    lax.fori_loop(0, n, ends, 0)
+
+    @pl.when(me == 0)
+    def _():
+        fin[...] = jnp.zeros_like(fin)
+
+    pl.semaphore_wait(barrier, n - 1)
+
+    def chain(c):
+        return pltpu.make_async_remote_copy(
+            src_ref=fout.at[c],
+            dst_ref=fin.at[c],
+            send_sem=chain_send.at[c],
+            recv_sem=chain_recv.at[c],
+            device_id={"ctx": lax.rem(me + 1, n)},
+            device_id_type=pl.DeviceIdType.MESH,
+        )
+
+    def outward(source, target, sends, recvs, there, slot):
+        return pltpu.make_async_remote_copy(
+            src_ref=source.at[there],
+            dst_ref=target.at[pl.ds(slot * groups, groups)] if target is got else target.at[slot],
+            send_sem=sends.at[there],
+            recv_sem=recvs.at[slot],
+            device_id={"ctx": there},
+            device_id_type=pl.DeviceIdType.MESH,
+        )
+
+    def one(c, carry):
+        @pl.when(me > 0)
+        def _():
+            chain(c).wait_recv()
+
+        state = fin[c].astype(jnp.float32)
+
+        @pl.when(me < n - 1)
+        def _():
+            fout[c] = (decay_s[c][0:1] * state + total_s[c]).astype(jnp.bfloat16)
+            chain(c).start()
+
+        def put(g, value):
+            made[c, g] = value
+
+        gated_chunk(c, state, put, x_ref, gate_ref, read_ref, starts_ref, *scratch)
+
+        @pl.when(c != me)
+        def _():
+            outward(made, got, send1, recv1, c, me).start()
+
+        @pl.when(c == me)
+        def _():
+            for g in range(groups):
+                got[me * groups + g] = made[c, g]
+
+        return carry
+
+    lax.fori_loop(0, n, one, 0)
+    for off in offsets:
+        there = lax.rem(me + off, n)
+        outward(made, got, send1, recv1, there, there).wait_recv()
+    for off in offsets:
+        there = lax.rem(me + off, n)
+        for g in range(groups):
+            stage[there, g] = got[order_ref[there * groups + g]]
+        outward(stage, final, send2, recv2, there, me).start()
+    for g in range(groups):
+        final[me, g] = got[order_ref[me * groups + g]]
+
+    @pl.when(me < n - 1)
+    def _():
+        for c in range(n):
+            chain(c).wait_send()
+
+    for off in offsets:
+        there = lax.rem(me + off, n)
+        outward(made, got, send1, recv1, there, there).wait_send()
+        outward(stage, final, send2, recv2, there, there).wait_send()
+    for off in offsets:
+        there = lax.rem(me + off, n)
+        outward(stage, final, send2, recv2, there, there).wait_recv()
+    tile = 32
+    for g in range(groups):
+
+        def norm(r, carry):
+            at = pl.ds(pl.multiple_of(r * tile, tile), tile)
+            total = jnp.zeros((tile, 1), jnp.float32)
+            for s in range(n):
+                v = final[s, g, at, :].astype(jnp.float32)
+                total = total + jnp.sum(v * v, axis=1, keepdims=True)
+            scale = lax.rsqrt(total * (1.0 / (n * WIDE)) + 1e-05)
+            for s in range(n):
+                v = final[s, g, at, :].astype(jnp.float32)
+                w = weight_ref[:, s * WIDE : (s + 1) * WIDE]
+                into = pl.ds(pl.multiple_of(g * GROUP + r * tile, tile), tile)
+                out_ref[into, s * WIDE : (s + 1) * WIDE] = (v * scale * w).astype(jnp.bfloat16)
+            return carry
+
+        lax.fori_loop(0, GROUP // tile, norm, 0)
 
 
 def norm_kernel(in_ref, weight_ref, out_ref):
@@ -256,6 +423,12 @@
         pltpu.VMEM((groups, chunks, GROUP, CHUNK), jnp.float32),
         pltpu.VMEM((groups, state_size, GROUP), jnp.bfloat16),
     ]
+    more = [
+        pltpu.VMEM((groups, chunks, CHUNK, GROUP), jnp.float32),
+        pltpu.VMEM((groups, chunks, CHUNK, GROUP), jnp.float32),
+        pltpu.VMEM((chunks, 8, CHUNK), jnp.float32),
+        pltpu.VMEM((groups, GROUP, GROUP), jnp.float32),
+    ]
     bias, dlog, gain = (v.reshape(1, -1) for v in (step_bias, decay_log, skip_gain))
 
     def to_owners(v):
@@ -267,6 +440,45 @@
         if not direct:
             v = v.transpose(1, 0, 2).reshape(1, v.shape[1], features)
         return v
+
+    if width == WIDE:
+        all_order = lax.all_gather(block_order, "ctx", axis=0, tiled=True)
+        slab = (devices, groups, GROUP, WIDE)
+        return pl.pallas_call(
+            functools.partial(fused_kernel, devices),
+            out_shape=jax.ShapeDtypeStruct((rows, features), jnp.bfloat16),
+            in_specs=[VM] * 9 + [SM] * 2,
+            out_specs=VM,
+            scratch_shapes=[
+                pltpu.VMEM((devices, state_size, WIDE), jnp.bfloat16),
+                pltpu.VMEM((devices, state_size, WIDE), jnp.bfloat16),
+                pltpu.VMEM((devices, state_size, WIDE), jnp.float32),
+                pltpu.VMEM((devices, 8, WIDE), jnp.float32),
+                pltpu.VMEM(slab, jnp.bfloat16),
+                pltpu.VMEM((devices * groups, GROUP, WIDE), jnp.bfloat16),
+                pltpu.VMEM(slab, jnp.bfloat16),
+                pltpu.VMEM(slab, jnp.bfloat16),
+            ]
+            + [pltpu.SemaphoreType.DMA((devices,))] * 6
+            + common
+            + more,
+            compiler_params=pltpu.CompilerParams(
+                collective_id=0, has_side_effects=True, vmem_limit_bytes=56 * 1024 * 1024
+            ),
+            name="fused",
+        )(
+            head_input,
+            gate_input,
+            increment_preactivation,
+            write_vector,
+            read_vector,
+            bias,
+            dlog,
+            gain,
+            norm_weight.reshape(1, -1),
+            doc_starts,
+            all_order,
+        )
 
     ends = pl.pallas_call(
         state_kernel,
@@ -294,12 +506,7 @@
         in_specs=[VM] * 9 + [SM],
         out_specs=VM,
         scratch_shapes=common
-        + [
-            pltpu.VMEM((groups, chunks, CHUNK, GROUP), jnp.float32),
-            pltpu.VMEM((groups, chunks, CHUNK, GROUP), jnp.float32),
-            pltpu.VMEM((chunks, 8, CHUNK), jnp.float32),
-            pltpu.VMEM((groups, GROUP, GROUP), jnp.float32),
-        ],
+        + more,
         compiler_params=limit,
         name="gated",
     )(

time: 198 us -> 193 us (0.975)
  Pallas kernels: 21.5 us -> 172 us
  blocking collectives: 117 us -> 13.6 us
  waiting for transfers between devices: 47.7 us -> 0 us
  starting transfers between devices: 3.6 us -> 0 us
    pallas_call x4 -> x1, Pallas kernels: 21.5 us -> 172 us  [local(): pl.pallas_call(functools.partial(fused_kernel, devices), out_shape=jax.Sh...]
    all_to_all x3 -> x0, blocking collectives: 117 us -> none  [the longest x1 52.1 us: local(): lax.all_to_all(blocks.reshape(devices, rows, width), 'ctx', split_axis=0,...]
    all_to_all x1 -> x0, waiting for transfers between devices: 47.7 us -> none  [to_owners(): return lax.all_to_all(v, 'ctx', split_axis=0, concat_axis=0, tiled=True)]
    unnamed x0 -> x1, blocking collectives: none -> 13.6 us
    all_to_all x1 -> x0, starting transfers between devices: 3.6 us -> none  [to_owners(): return lax.all_to_all(v, 'ctx', split_axis=0, concat_axis=0, tiled=True)]
    gather x1 -> x0, local copies, waits for them, and re-layouts: 2 us -> none  [local(): blocks = gated.reshape(devices * groups, GROUP, width)[all_order]]
    unnamed x27 -> x5, local copies, waits for them, and re-layouts: 5.95 us -> 6.72 us
  transfers between devices with their start and end apart: 1 -> 0, of which waited for: 1 -> 0; matrix products, arithmetic and copies ran while one was open for 0% -> 0% of each run, Pallas kernels for 0% -> 0%
where the time goes in v1:
time: 193 us
  Pallas kernels  172 us (89%)
  blocking collectives  13.6 us (7%)
  local copies, waits for them, and re-layouts  6.72 us (3%)
    pallas_call x1, Pallas kernels, local(): pl.pallas_call(functools.partial(fused_kernel, devices), out_shape=jax.Sh...  172 us
    unnamed x1, blocking collectives  13.6 us
    unnamed x5, local copies, waits for them, and re-layouts  6.72 us

profile of v1, /device:TPU:0, one launch (start us, length us, event | category | flops | bytes accessed | tf_op | source)
XLA Modules:
  0.0 192.9 jit_solution(17464029881932299165)
XLA Ops:
  0.0 1.2 dynamic-slice
  1.9 0.9 dynamic-update-slice
  2.8 13.6 %all-reduce.order_ref = s32[16]{0:T(128)} all-reduce(s32[16]{0:T(128)S(1)} %dynamic-update-slice), channel_id=1, replica_groups=mesh['ctx'=8,'dp'=4] {'ctx'}, use_global_device_ids=true, to_apply=%add | all-reduce | flops 16 | bytes 128
  16.4 1.5 copy.12.logit_ref
  17.8 171.9 %fused.1 = bf16[256,4096]{1,0:T(8,128)(2,1)} custom-call(bf16[256,4096]{1,0:T(8,128)(2,1)} %x_ref.1, bf16[256,4096]{1,0:T(8,128)(2,1)} %gate_ref.1, bf16[256,64]{1,0:T(8,128)(2,1)} %copy.12.logit_ref, bf16[256,128]{1,0:T(8,128)(2,1)} %write_ref.1, bf16[256,128]{1,0:T(8,128)(2,1)} %read_ref.1, f32[1,64]{1,0:T(1,128)} %bitcast.6, f32[1,64]{1,0:T(1,128)} %bitcast.7, ...), custom_call_target="tpu_custom_call" | custom-call | tf_op jit(solution)/shard_map/fused/pallas_call | solution.py:447
  189.8 3.1 %copy.15 = bf16[256,4096]{1,0:T(8,128)(2,1)} copy(bf16[256,4096]{1,0:T(8,128)(2,1)} %fused.1) | data formatting | bytes 4194304
  (1 shorter events, 0.0 us)

commit v2 on v1

--- a/solution.py
+++ b/solution.py
@@ -249,18 +249,70 @@
     recv1,
     send2,
     recv2,
+    send3,
+    recv3,
+    order_all,
+    order_s,
+    order_sem,
     *scratch,
 ):
     cum_s, dt_s, write_t = scratch[:3]
     groups = cum_s.shape[0]
     me = lax.axis_index("ctx")
-    offsets = sorted(range(1, n), key=lambda k: abs(k - n // 2))
+    offsets = range(1, n)
+    half = n // 2
+    mine = (me // half) * half
+    other = half - mine
+
+    def partner(k):
+        far = 1 - k % 2
+        return far * other + (1 - far) * mine + lax.rem(me + k // 2, half)
+
     barrier = pltpu.get_barrier_semaphore()
     for off in range(1, n):
         pl.semaphore_signal(
             barrier, inc=1, device_id={"ctx": lax.rem(me + off, n)}, device_id_type=pl.DeviceIdType.MESH
         )
     gated_setup(logit_ref, bias_ref, dlog_ref, write_ref, read_ref, gain_ref, *scratch)
+
+    @pl.when(me == 0)
+    def _():
+        fin[...] = jnp.zeros_like(fin)
+
+    def chain(c):
+        return pltpu.make_async_remote_copy(
+            src_ref=fout.at[c],
+            dst_ref=fin.at[c],
+            send_sem=chain_send.at[c],
+            recv_sem=chain_recv.at[c],
+            device_id={"ctx": lax.rem(me + 1, n)},
+            device_id_type=pl.DeviceIdType.MESH,
+        )
+
+    def spread_order(there, slot):
+        return pltpu.make_async_remote_copy(
+            src_ref=order_ref,
+            dst_ref=order_all.at[slot],
+            send_sem=send3.at[there],
+            recv_sem=recv3.at[slot],
+            device_id={"ctx": there},
+            device_id_type=pl.DeviceIdType.MESH,
+        )
+
+    def outward(source, target, sends, recvs, there, slot):
+        return pltpu.make_async_remote_copy(
+            src_ref=source.at[there],
+            dst_ref=target.at[pl.ds(slot * groups, groups)] if target is got else target.at[slot],
+            send_sem=sends.at[there],
+            recv_sem=recvs.at[slot],
+            device_id={"ctx": there},
+            device_id_type=pl.DeviceIdType.MESH,
+        )
+
+    pl.semaphore_wait(barrier, n - 1)
+    order_all[me] = order_ref[...]
+    for off in offsets:
+        spread_order(lax.rem(me + off, n), me).start()
 
     def ends(c, carry):
         cols = pl.ds(pl.multiple_of(c * WIDE, WIDE), WIDE)
@@ -273,47 +325,34 @@
             decay = factor if decay is None else factor * decay
         total_s[c] = total
         decay_s[c] = jnp.broadcast_to(decay, (8, WIDE))
+
+        @pl.when(me == 0)
+        def _():
+            fout[c] = total.astype(jnp.bfloat16)
+            chain(c).start()
+
         return carry
 
     lax.fori_loop(0, n, ends, 0)
 
-    @pl.when(me == 0)
-    def _():
-        fin[...] = jnp.zeros_like(fin)
-
-    pl.semaphore_wait(barrier, n - 1)
-
-    def chain(c):
-        return pltpu.make_async_remote_copy(
-            src_ref=fout.at[c],
-            dst_ref=fin.at[c],
-            send_sem=chain_send.at[c],
-            recv_sem=chain_recv.at[c],
-            device_id={"ctx": lax.rem(me + 1, n)},
-            device_id_type=pl.DeviceIdType.MESH,
-        )
-
-    def outward(source, target, sends, recvs, there, slot):
-        return pltpu.make_async_remote_copy(
-            src_ref=source.at[there],
-            dst_ref=target.at[pl.ds(slot * groups, groups)] if target is got else target.at[slot],
-            send_sem=sends.at[there],
-            recv_sem=recvs.at[slot],
-            device_id={"ctx": there},
-            device_id_type=pl.DeviceIdType.MESH,
-        )
-
-    def one(c, carry):
-        @pl.when(me > 0)
-        def _():
-            chain(c).wait_recv()
-
-        state = fin[c].astype(jnp.float32)
+    def relay(c, carry):
+        chain(c).wait_recv()
 
         @pl.when(me < n - 1)
         def _():
+            state = fin[c].astype(jnp.float32)
             fout[c] = (decay_s[c][0:1] * state + total_s[c]).astype(jnp.bfloat16)
             chain(c).start()
+
+        return carry
+
+    @pl.when(me > 0)
+    def _():
+        lax.fori_loop(0, n, relay, 0)
+
+    def one(k, carry):
+        c = partner(k)
+        state = fin[c].astype(jnp.float32)
 
         def put(g, value):
             made[c, g] = value
@@ -334,14 +373,28 @@
     lax.fori_loop(0, n, one, 0)
     for off in offsets:
         there = lax.rem(me + off, n)
-        outward(made, got, send1, recv1, there, there).wait_recv()
+        spread_order(there, there).wait_recv()
+    fetch = pltpu.make_async_copy(order_all, order_s, order_sem)
+    fetch.start()
+    fetch.wait()
     for off in offsets:
         there = lax.rem(me + off, n)
+        outward(made, got, send1, recv1, there, there).wait_recv()
+
+    def second(k, carry):
+        there = partner(k)
         for g in range(groups):
-            stage[there, g] = got[order_ref[there * groups + g]]
-        outward(stage, final, send2, recv2, there, me).start()
+            stage[there, g] = got[order_s[there, 0, g]]
+
+        @pl.when(there != me)
+        def _():
+            outward(stage, final, send2, recv2, there, me).start()
+
+        return carry
+
+    lax.fori_loop(0, n, second, 0)
     for g in range(groups):
-        final[me, g] = got[order_ref[me * groups + g]]
+        final[me, g] = stage[me, g]
 
     @pl.when(me < n - 1)
     def _():
@@ -352,6 +405,7 @@
         there = lax.rem(me + off, n)
         outward(made, got, send1, recv1, there, there).wait_send()
         outward(stage, final, send2, recv2, there, there).wait_send()
+        spread_order(there, there).wait_send()
     for off in offsets:
         there = lax.rem(me + off, n)
         outward(stage, final, send2, recv2, there, there).wait_recv()
@@ -441,13 +495,13 @@
             v = v.transpose(1, 0, 2).reshape(1, v.shape[1], features)
         return v
 
-    if width == WIDE:
-        all_order = lax.all_gather(block_order, "ctx", axis=0, tiled=True)
+    if width == WIDE and devices % 2 == 0:
+        order = jnp.broadcast_to(jnp.pad(block_order, (0, 128 - groups))[None], (8, 128))
         slab = (devices, groups, GROUP, WIDE)
         return pl.pallas_call(
             functools.partial(fused_kernel, devices),
             out_shape=jax.ShapeDtypeStruct((rows, features), jnp.bfloat16),
-            in_specs=[VM] * 9 + [SM] * 2,
+            in_specs=[VM] * 9 + [SM, VM],
             out_specs=VM,
             scratch_shapes=[
                 pltpu.VMEM((devices, state_size, WIDE), jnp.bfloat16),
@@ -459,7 +513,12 @@
                 pltpu.VMEM(slab, jnp.bfloat16),
                 pltpu.VMEM(slab, jnp.bfloat16),
             ]
-            + [pltpu.SemaphoreType.DMA((devices,))] * 6
+            + [pltpu.SemaphoreType.DMA((devices,))] * 8
+            + [
+                pltpu.VMEM((devices, 8, 128), jnp.int32),
+                pltpu.SMEM((devices, 8, 128), jnp.int32),
+                pltpu.SemaphoreType.DMA,
+            ]
             + common
             + more,
             compiler_params=pltpu.CompilerParams(
@@ -477,7 +536,7 @@
             gain,
             norm_weight.reshape(1, -1),
             doc_starts,
-            all_order,
+            order,
         )
 
     ends = pl.pallas_call(

time: 193 us -> 173 us (0.90)
  blocking collectives: 13.6 us -> 0 us
  Pallas kernels: 172 us -> 167 us
    unnamed x1 -> x0, blocking collectives: 13.6 us -> none
    pallas_call x1, Pallas kernels: 172 us -> 167 us  [local(): pl.pallas_call(functools.partial(fused_kernel, devices), out_shape=jax.Sh...]
    unnamed x5 -> x2, local copies, waits for them, and re-layouts: 6.72 us -> 4.62 us
where the time goes in v2:
time: 173 us
  Pallas kernels  167 us (97%)
  local copies, waits for them, and re-layouts  5.88 us (3%)
    pallas_call x1, Pallas kernels, local(): pl.pallas_call(functools.partial(fused_kernel, devices), out_shape=jax.Sh...  167 us
    unnamed x2, local copies, waits for them, and re-layouts  4.62 us

profile of v2, /device:TPU:0, one launch (start us, length us, event | category | flops | bytes accessed | tf_op | source)
XLA Modules:
  0.0 173.0 jit_solution(15754723835029018646)
XLA Ops:
  0.0 0.7 pad.4
  0.7 0.6 broadcast_in_dim.2.order_ref
  1.3 1.5 copy.12.logit_ref
  2.7 167.1 %fused.1 = bf16[256,4096]{1,0:T(8,128)(2,1)} custom-call(bf16[256,4096]{1,0:T(8,128)(2,1)} %x_ref.1, bf16[256,4096]{1,0:T(8,128)(2,1)} %gate_ref.1, bf16[256,64]{1,0:T(8,128)(2,1)} %copy.12.logit_ref, bf16[256,128]{1,0:T(8,128)(2,1)} %write_ref.1, bf16[256,128]{1,0:T(8,128)(2,1)} %read_ref.1, f32[1,64]{1,0:T(1,128)} %bitcast.5, f32[1,64]{1,0:T(1,128)} %bitcast.6, ...), custom_call_target="tpu_custom_call" | custom-call | tf_op jit(solution)/shard_map/fused/pallas_call | solution.py:501
  169.9 3.1 %copy.14 = bf16[256,4096]{1,0:T(8,128)(2,1)} copy(bf16[256,4096]{1,0:T(8,128)(2,1)} %fused.1) | data formatting | bytes 4194304
